TPU v7x, 128 devices: a whole 4x4x4 slice. The times are simulated.
128 devices in a mesh: dp: 8 (over x, core), pipe: 4 (over y), tensor: 4 (over z).
Axes of the slice: x: 4, y: 4, z: 4, core: 2. Of those that a mesh axis runs over, the one named last changes fastest.
Arguments:
- support_tokens: int32 [64, 32], P(('dp', 'pipe')), may hold values from 0 to 64127
- support_lengths: int32 [64], P(('dp', 'pipe')), may hold values from 1 to 32
- support_labels: int32 [64, 1], P(('dp', 'pipe')), may hold values from 0 to 31
- query_tokens: int32 [32, 32], P(('dp', 'pipe')), may hold values from 0 to 64127
- query_lengths: int32 [32], P(('dp', 'pipe')), may hold values from 1 to 32
- query_episodes: int32 [32], P(('dp', 'pipe')), may hold values from 0 to 1
- embedding: bfloat16 [64128, 4096], P(('dp', 'pipe'), 'tensor'), may hold values from -18 to 18
- attn_gain: float32 [4, 4096], P('pipe'), may hold values from 0.5 to 1.5
- query_weight: bfloat16 [4, 4096, 4096], P('pipe', None, 'tensor'), may hold values from -1 to 1
- key_weight: bfloat16 [4, 4096, 1024], P('pipe', None, 'tensor'), may hold values from -16 to 16
- value_weight: bfloat16 [4, 4096, 1024], P('pipe', None, 'tensor'), may hold values from -0.09375 to 0.09375
- out_weight: bfloat16 [4, 4096, 4096], P('pipe', 'tensor'), may hold values from -0.09375 to 0.09375
- final_gain: float32 [4096], replicated, may hold values from 0.5 to 1.5
Outputs:
- prototypes: float32 [32, 4096], P(None, 'tensor')
- logits: float32 [32, 16], P(('dp', 'pipe'))
Inputs may be any that keep to these rules, and one draw needn't show every extreme that they name: `support_labels`: every class is the label of at least one support sequence.
All inputs are finite; a program needn't handle non-finite values.
Results may differ from a plain program's by a relative error of at most 0.024.
Values may be sent and summed in bfloat16 or wider, within the bound.
A program may use at most 128 MiB of HBM per device.

v0:
```python
import math

import jax
import jax.numpy as jnp
from jax import lax
from jax.sharding import PartitionSpec as P

D = 4096
HEAD_DIM = 128
WAYS = 16
EPISODES = 2


epsilon = 1e-05
rotary_base = 500000.0


def in_order(blocks, dim):
    blocks = jnp.moveaxis(blocks, 0, dim)
    dims = blocks.shape
    return blocks.reshape(*dims[:dim], dims[dim] * dims[dim + 1], *dims[dim + 2 :])


def sent_to_all(shard, axis):
    copies = jnp.broadcast_to(shard, (lax.axis_size(axis), *shard.shape))
    return lax.all_to_all(copies, axis, split_axis=0, concat_axis=0, tiled=True)


def collect(shard, axis, dim):
    return in_order(sent_to_all(shard, axis), dim)


def split_up(shard, dim, length):
    dims = shard.shape
    blocks = shard.reshape(*dims[:dim], length, dims[dim] // length, *dims[dim + 1 :])
    return jnp.moveaxis(blocks, dim, 0)


def sum_at_owner(shard, axis, dim):
    length = lax.axis_size(axis)
    blocks = lax.all_to_all(split_up(shard, dim, length), axis, 0, 0, tiled=True)
    return jnp.sum(blocks.astype(jnp.float32), axis=0)


def passed_along(block, axis, distance):
    devices = range(lax.axis_size(axis))
    route = [((i - distance) % len(devices), i) for i in devices]
    return lax.ppermute(block, axis, route)


def over_copies(shard, axis):
    return sent_to_all(shard, axis).astype(jnp.float32).sum(axis=0)


def rotate(heads_in, seq_len):
    half_dim = HEAD_DIM // 2
    freqs = jnp.exp(
        -math.log(rotary_base) * jnp.arange(half_dim, dtype=jnp.float32) * (2.0 / HEAD_DIM)
    )
    angles = jnp.arange(seq_len, dtype=jnp.float32)[:, None] * freqs[None, :]
    cosine = jnp.cos(angles)[None, :, None, :]
    sine = jnp.sin(angles)[None, :, None, :]
    first_half = heads_in[..., :half_dim]
    second_half = heads_in[..., half_dim:]
    return jnp.concatenate(
        [first_half * cosine - second_half * sine, second_half * cosine + first_half * sine],
        axis=-1,
    )


def whole_rows(hidden):
    return collect(hidden, "tensor", 1)


def whole_values(full_rows, gain_vector):
    values = full_rows.astype(jnp.float32)
    mean_square = jnp.mean(values * values, axis=-1, keepdims=True)
    return values * lax.rsqrt(mean_square + epsilon) * gain_vector


def shards(
    support_tokens,
    support_lengths,
    support_labels,
    query_tokens,
    query_lengths,
    query_episodes,
    embedding,
    attn_gain,
    query_weight,
    key_weight,
    value_weight,
    out_weight,
    final_gain,
):
    group_count = lax.axis_size(("dp", "pipe"))
    sections = lax.axis_size("pipe")
    sup_dev, seq_len = support_tokens.shape
    qry_dev = query_tokens.shape[0]
    seq_count = sup_dev + qry_dev
    row_count = seq_count * seq_len
    table_rows, width = embedding.shape
    column_start = lax.axis_index("tensor") * width
    all_support, all_query, every_sup_len, every_qry_len = (
        lax.all_gather(support_tokens, ("dp", "pipe"), axis=0, tiled=True),
        lax.all_gather(query_tokens, ("dp", "pipe"), axis=0, tiled=True),
        lax.all_gather(support_lengths, ("dp", "pipe"), axis=0, tiled=True),
        lax.all_gather(query_lengths, ("dp", "pipe"), axis=0, tiled=True),
    )
    token_flat = jnp.concatenate(
        [all_support.reshape(group_count, sup_dev * seq_len), all_query], axis=1
    ).reshape(group_count * row_count)
    local_ids = token_flat - lax.axis_index(("dp", "pipe")) * table_rows
    inside = (local_ids >= 0) & (local_ids < table_rows)
    picked = jnp.take(embedding, jnp.clip(local_ids, 0, table_rows - 1), axis=0)
    picked = jnp.where(inside[:, None], picked, jnp.zeros_like(picked))
    replies = lax.all_to_all(picked, ("dp", "pipe"), split_axis=0, concat_axis=0, tiled=True)
    hidden = jnp.sum(
        replies.reshape(group_count, row_count, width).astype(jnp.float32), axis=0
    ).astype(jnp.bfloat16)
    seq_lengths = jnp.concatenate([support_lengths, query_lengths], axis=0)
    query_proj = query_weight[0]
    key_proj = key_weight[0]
    value_proj = value_weight[0]
    out_proj = out_weight[0]
    gain_vector = attn_gain[0]
    local_heads = query_proj.shape[1] // HEAD_DIM
    local_groups = key_proj.shape[1] // HEAD_DIM
    group_size = local_heads // local_groups
    w_in = jnp.concatenate([query_proj, key_proj, value_proj], axis=1)
    query_cols = local_heads * HEAD_DIM
    key_cols = local_groups * HEAD_DIM
    positions = jnp.arange(seq_len)
    causal = positions[None, :] <= positions[:, None]

    def section_block(stream, lengths_here):
        normed = whole_values(whole_rows(stream), gain_vector).astype(jnp.bfloat16)
        projected = jnp.dot(normed, w_in, preferred_element_type=jnp.float32)
        query_heads = projected[:, :query_cols].reshape(seq_count, seq_len, local_heads, HEAD_DIM)
        key_heads = projected[:, query_cols : query_cols + key_cols].reshape(
            seq_count, seq_len, local_groups, HEAD_DIM
        )
        value_heads = (
            projected[:, query_cols + key_cols :]
            .reshape(seq_count, seq_len, local_groups, HEAD_DIM)
            .astype(jnp.bfloat16)
        )
        query_heads = (
            rotate(query_heads, seq_len)
            .astype(jnp.bfloat16)
            .reshape(seq_count, seq_len, local_groups, group_size, HEAD_DIM)
        )
        key_heads = rotate(key_heads, seq_len).astype(jnp.bfloat16)
        scores = jnp.einsum(
            "sikgd,sjkd->skgij", query_heads, key_heads, preferred_element_type=jnp.float32
        ) / math.sqrt(HEAD_DIM)
        visible = causal[None, :, :] & (positions[None, None, :] < lengths_here[:, None, None])
        scores = jnp.where(visible[:, None, None, :, :], scores, -1e30)
        weights = jax.nn.softmax(scores, axis=-1).astype(jnp.bfloat16)
        mixed = jnp.einsum(
            "skgij,sjkd->sikgd", weights, value_heads, preferred_element_type=jnp.float32
        )
        mixed = mixed.astype(jnp.bfloat16).reshape(row_count, query_cols)
        partial_out = jnp.dot(mixed, out_proj, preferred_element_type=jnp.float32)
        summed = sum_at_owner(partial_out.astype(jnp.bfloat16), "tensor", 1)
        return (stream.astype(jnp.float32) + summed).astype(jnp.bfloat16)

    section_index = lax.axis_index("pipe")
    dp_base = lax.axis_index("dp") * sections

    def tick(tick_index, stream):
        held_group = dp_base + (section_index - tick_index) % sections
        sup_part = lax.dynamic_slice_in_dim(every_sup_len, held_group * sup_dev, sup_dev)
        qry_part = lax.dynamic_slice_in_dim(every_qry_len, held_group * qry_dev, qry_dev)
        lengths_here = jnp.concatenate([sup_part, qry_part], axis=0)
        first_tick = (tick_index - section_index) % sections
        active = (first_tick <= tick_index) & (tick_index < first_tick + sections)
        computed = section_block(stream, lengths_here)
        stream = jnp.where(active, computed, stream)
        return passed_along(stream, "pipe", 1)

    hidden = lax.fori_loop(0, 2 * sections, tick, hidden)
    final = lax.dynamic_slice_in_dim(
        whole_values(whole_rows(hidden), final_gain), column_start, width, 1
    )
    live = (positions[None, :] < seq_lengths[:, None]).astype(jnp.float32)
    pooled = jnp.sum(
        final.reshape(seq_count, seq_len, width) * live[:, :, None], axis=1
    ) / seq_lengths[:, None].astype(jnp.float32)
    support_pooled = pooled[:sup_dev]
    query_pooled = pooled[sup_dev:]
    class_count_all = EPISODES * WAYS
    onehot = (support_labels[:, 0][:, None] == jnp.arange(class_count_all)[None, :]).astype(
        jnp.float32
    )
    class_total = jnp.dot(onehot.T, support_pooled, precision=lax.Precision.HIGHEST)
    class_count = jnp.sum(onehot, axis=0)
    class_total, class_count = (
        over_copies(class_total.astype(jnp.bfloat16), ("dp", "pipe")).astype(jnp.float32),
        over_copies(class_count.astype(jnp.bfloat16), ("dp", "pipe")).astype(jnp.float32),
    )
    prototypes = class_total / class_count[:, None]
    episode_pick = (query_episodes[:, None] == jnp.arange(EPISODES)[None, :]).astype(jnp.float32)
    chosen = jnp.einsum(
        "qe,ewc->qwc",
        episode_pick,
        prototypes.reshape(EPISODES, WAYS, width),
        precision=lax.Precision.HIGHEST,
    )
    partial_distance = jnp.sum((query_pooled[:, None, :] - chosen) ** 2, axis=-1)
    distance = lax.psum(partial_distance, "tensor")
    logits = -distance / math.sqrt(D)
    return (prototypes, logits)


def solution(mesh):
    return jax.shard_map(
        shards,
        mesh=mesh,
        in_specs=(
            P(("dp", "pipe"), None),
            P(("dp", "pipe")),
            P(("dp", "pipe"), None),
            P(("dp", "pipe"), None),
            P(("dp", "pipe")),
            P(("dp", "pipe")),
            P(("dp", "pipe"), "tensor"),
            P("pipe", None),
            P("pipe", None, "tensor"),
            P("pipe", None, "tensor"),
            P("pipe", None, "tensor"),
            P("pipe", "tensor", None),
            P(),
        ),
        out_specs=(P(None, "tensor"), P(("dp", "pipe"), None)),
        check_vma=False,
    )
```

profile of v0, /device:TPU:1, one launch (start us, length us, event | category | flops | bytes accessed | tf_op | source)
XLA Modules:
  0.0 679.7 jit_solution(12424556584828293104)
XLA Ops:
  0.6 34.1 %all-gather.1 = s32[32,1,32]{2,1,0:T(1,128)S(1)} all-gather(s32[1,1,32]{2,1,0:T(1,128)} %bitcast.148), channel_id=1, replica_groups=mesh['dp'=8,'pipe'=4,'tensor'=4] {'dp','pipe'}, dimensions={0}, use_global_device_ids=true | all-gather | bytes 4224 | tf_op jit(solution)/shard_map/all_gather | solution.py:106
  34.7 37.0 %all-gather = s32[32,2,32]{2,1,0:T(2,128)S(1)} all-gather(s32[1,2,32]{2,1,0:T(2,128)} %bitcast.144), channel_id=1, replica_groups=mesh['dp'=8,'pipe'=4,'tensor'=4] {'dp','pipe'}, dimensions={0}, use_global_device_ids=true | all-gather | bytes 8448 | tf_op jit(solution)/shard_map/all_gather | solution.py:105
  72.0 18.7 %gather_fusion = bf16[3072,1024]{1,0:T(8,128)(2,1)} fusion(bf16[2004,1024]{1,0:T(8,128)(2,1)} %param.21, s32[3072]{0:T(1024)S(1)} %broadcast_clamp_fusion.1), kind=kCustom, calls=%fused_computation | custom fusion | bytes 12595200 | tf_op jit(solution)/shard_map/jit(_take)/gather | solution.py:115
  90.6 7.0 %select_select_fusion = bf16[32,96,1024]{2,1,0:T(8,128)(2,1)} fusion(bf16[32,96,1024]{2,1,0:T(8,128)(2,1)} %bitcast.128, pred[32,96]{1,0:T(8,128)(4,1)S(1)} %get-tuple-element.312, pred[32,96]{1,0:T(8,128)(4,1)S(1)} %get-tuple-element.322), kind=kLoop, calls=%fused_computation.56 | loop fusion | flops 6291456 | bytes 12589056 | tf_op jit(solution)/shard_map/jit(_where)/select_n | solution.py:116
  97.6 6.1 all-to-all-start.2
  106.8 78.8 %all-reduce.2 = (s32[64]{0:T(128)S(1)}, s32[32]{0:T(128)S(1)}) all-reduce(s32[64]{0:T(128)S(1)} %dynamic-update-slice, s32[32]{0:T(128)S(1)} %dynamic-update-slice.1), channel_id=1, replica_groups=mesh['dp'=8,'pipe'=4,'tensor'=4] {'dp','pipe'}, use_global_device_ids=true, to_apply=%add | all-reduce | flops 96 | bytes 768
  185.6 11.6 %pad_maximum_fusion = bf16[4096,1536]{1,0:T(8,128)(2,1)} fusion(bf16[4096,256]{1,0:T(8,128)(2,1)S(1)} %bitcast.135, bf16[4096,256]{1,0:T(8,128)(2,1)} %bitcast.136, bf16[4096,1024]{1,0:T(8,128)(2,1)} %bitcast.129), kind=kLoop, calls=%fused_computation.55 | loop fusion | flops 37748736 | bytes 25165824 | tf_op jit(solution)/shard_map/concatenate | solution.py:130
  201.4 382.3 %while.16 = (s32[]{:T(128)}, bf16[96,1024]{1,0:T(8,128)(2,1)S(1)}, s32[]{:T(128)}, f32[1,4096]{1,0:T(1,128)S(1)}, bf16[4096,1536]{1,0:T(8,128)(2,1)}, /*index=5*...) while((s32[]{:T(128)}, bf16[96,1024]{1,0:T(8,128)(2,1)S(1)}, ...), condition=%wide.region_6.7_spmd.clone, body=%wide.region_1.0_spmd.clone.sunk | while | flops 2038168704 | bytes 45535072 | solution.py:182
  202.5 5.0 all-to-all-start
  209.2 9.3 %all-to-all-done = bf16[4,96,1024]{2,1,0:T(8,128)(2,1)S(1)} async-done(((bf16[4,96,1024]{2,1,0:T(8,128)(2,1)}), bf16[4,96,1024]{2,1,0:T(8,128)(2,1)S(1)}, u32[]{:S(2)}, u32[]{:S(2)}) %all-to-all-start) | async-done | bytes 786464 | tf_op jit(solution)/shard_map/while/body/eval_jaxpr/all_to_all | solution.py:26
  219.1 6.8 fusion.84
  228.1 4.8 convolution_convert_fusion.4
  237.5 9.8 %all-to-all-done.1 = bf16[4,96,1024]{2,1,0:T(8,128)(2,1)S(1)} async-done(((bf16[4,96,1024]{2,1,0:T(8,128)(2,1)}), bf16[4,96,1024]{2,1,0:T(8,128)(2,1)S(1)}, u32[]{:S(2)}, u32[]{:S(2)}) %all-to-all-start.1) | async-done | bytes 786464 | tf_op jit(solution)/shard_map/while/body/eval_jaxpr/all_to_all | solution.py:41
  259.6 6.5 all-to-all-done
  266.7 6.8 fusion.84
  275.7 4.8 convolution_convert_fusion.4
  285.1 8.3 %all-to-all-done.1 = bf16[4,96,1024]{2,1,0:T(8,128)(2,1)S(1)} async-done(((bf16[4,96,1024]{2,1,0:T(8,128)(2,1)}), bf16[4,96,1024]{2,1,0:T(8,128)(2,1)S(1)}, u32[]{:S(2)}, u32[]{:S(2)}) %all-to-all-start.1) | async-done | bytes 786464 | tf_op jit(solution)/shard_map/while/body/eval_jaxpr/all_to_all | solution.py:41
  293.6 6.0 collective-permute-done
  305.9 6.5 all-to-all-done
  313.0 6.8 fusion.84
  331.4 8.3 %all-to-all-done.1 = bf16[4,96,1024]{2,1,0:T(8,128)(2,1)S(1)} async-done(((bf16[4,96,1024]{2,1,0:T(8,128)(2,1)}), bf16[4,96,1024]{2,1,0:T(8,128)(2,1)S(1)}, u32[]{:S(2)}, u32[]{:S(2)}) %all-to-all-start.1) | async-done | bytes 786464 | tf_op jit(solution)/shard_map/while/body/eval_jaxpr/all_to_all | solution.py:41
  340.0 6.0 collective-permute-done
  352.3 6.5 all-to-all-done
  359.3 6.8 fusion.84
  377.7 8.3 %all-to-all-done.1 = bf16[4,96,1024]{2,1,0:T(8,128)(2,1)S(1)} async-done(((bf16[4,96,1024]{2,1,0:T(8,128)(2,1)}), bf16[4,96,1024]{2,1,0:T(8,128)(2,1)S(1)}, u32[]{:S(2)}, u32[]{:S(2)}) %all-to-all-start.1) | async-done | bytes 786464 | tf_op jit(solution)/shard_map/while/body/eval_jaxpr/all_to_all | solution.py:41
  386.3 5.7 collective-permute-done
  398.3 6.5 all-to-all-done
  405.4 6.8 fusion.84
  414.4 4.8 convolution_convert_fusion.4
  423.8 8.3 %all-to-all-done.1 = bf16[4,96,1024]{2,1,0:T(8,128)(2,1)S(1)} async-done(((bf16[4,96,1024]{2,1,0:T(8,128)(2,1)}), bf16[4,96,1024]{2,1,0:T(8,128)(2,1)S(1)}, u32[]{:S(2)}, u32[]{:S(2)}) %all-to-all-start.1) | async-done | bytes 786464 | tf_op jit(solution)/shard_map/while/body/eval_jaxpr/all_to_all | solution.py:41
  432.3 5.7 collective-permute-done
  444.3 7.8 %all-to-all-done = bf16[4,96,1024]{2,1,0:T(8,128)(2,1)S(1)} async-done(((bf16[4,96,1024]{2,1,0:T(8,128)(2,1)}), bf16[4,96,1024]{2,1,0:T(8,128)(2,1)S(1)}, u32[]{:S(2)}, u32[]{:S(2)}) %all-to-all-start) | async-done | bytes 786464 | tf_op jit(solution)/shard_map/while/body/eval_jaxpr/all_to_all | solution.py:26
  452.7 6.8 fusion.84
  471.1 8.3 %all-to-all-done.1 = bf16[4,96,1024]{2,1,0:T(8,128)(2,1)S(1)} async-done(((bf16[4,96,1024]{2,1,0:T(8,128)(2,1)}), bf16[4,96,1024]{2,1,0:T(8,128)(2,1)S(1)}, u32[]{:S(2)}, u32[]{:S(2)}) %all-to-all-start.1) | async-done | bytes 786464 | tf_op jit(solution)/shard_map/while/body/eval_jaxpr/all_to_all | solution.py:41
  479.6 5.7 collective-permute-done
  491.7 10.5 %all-to-all-done = bf16[4,96,1024]{2,1,0:T(8,128)(2,1)S(1)} async-done(((bf16[4,96,1024]{2,1,0:T(8,128)(2,1)}), bf16[4,96,1024]{2,1,0:T(8,128)(2,1)S(1)}, u32[]{:S(2)}, u32[]{:S(2)}) %all-to-all-start) | async-done | bytes 786464 | tf_op jit(solution)/shard_map/while/body/eval_jaxpr/all_to_all | solution.py:26
  502.7 6.8 fusion.84
  521.1 8.3 %all-to-all-done.1 = bf16[4,96,1024]{2,1,0:T(8,128)(2,1)S(1)} async-done(((bf16[4,96,1024]{2,1,0:T(8,128)(2,1)}), bf16[4,96,1024]{2,1,0:T(8,128)(2,1)S(1)}, u32[]{:S(2)}, u32[]{:S(2)}) %all-to-all-start.1) | async-done | bytes 786464 | tf_op jit(solution)/shard_map/while/body/eval_jaxpr/all_to_all | solution.py:41
  529.7 5.7 collective-permute-done
  541.7 7.1 %all-to-all-done = bf16[4,96,1024]{2,1,0:T(8,128)(2,1)S(1)} async-done(((bf16[4,96,1024]{2,1,0:T(8,128)(2,1)}), bf16[4,96,1024]{2,1,0:T(8,128)(2,1)S(1)}, u32[]{:S(2)}, u32[]{:S(2)}) %all-to-all-start) | async-done | bytes 786464 | tf_op jit(solution)/shard_map/while/body/eval_jaxpr/all_to_all | solution.py:26
  549.3 6.8 fusion.84
  567.7 10.1 %all-to-all-done.1 = bf16[4,96,1024]{2,1,0:T(8,128)(2,1)S(1)} async-done(((bf16[4,96,1024]{2,1,0:T(8,128)(2,1)}), bf16[4,96,1024]{2,1,0:T(8,128)(2,1)S(1)}, u32[]{:S(2)}, u32[]{:S(2)}) %all-to-all-start.1) | async-done | bytes 786464 | tf_op jit(solution)/shard_map/while/body/eval_jaxpr/all_to_all | solution.py:41
  578.0 5.7 collective-permute-done
  588.5 8.0 %all-to-all-done.3 = bf16[4,96,1024]{2,1,0:T(8,128)(2,1)S(1)} async-done(((bf16[4,96,1024]{2,1,0:T(8,128)(2,1)}), bf16[4,96,1024]{2,1,0:T(8,128)(2,1)S(1)}, u32[]{:S(2)}, u32[]{:S(2)}) %all-to-all-start.3) | async-done | bytes 786464 | tf_op jit(solution)/shard_map/all_to_all | solution.py:26
  597.1 34.2 %all-to-all-start.5 = ((bf16[32,1,32]{2,1,0:T(2,128)(2,1)}), bf16[32,1,32]{2,1,0:T(2,128)(2,1)S(1)}, u32[]{:S(2)}, u32[]{:S(2)}) async-start(bf16[32,1,32]{2,1,0:T(2,128)(2,1)} %broadcast_in_dim.130), calls=%async_computation.5 | async-start | bytes 32768 | tf_op jit(solution)/shard_map/all_to_all | solution.py:26
  632.6 5.6 all-to-all-done.5
  644.9 26.4 %all-to-all-done.4 = bf16[32,32,1024]{2,1,0:T(8,128)(2,1)S(1)} async-done(((bf16[32,32,1024]{2,1,0:T(8,128)(2,1)}), bf16[32,32,1024]{2,1,0:T(8,128)(2,1)S(1)}, u32[]{:S(2)}, u32[]{:S(2)}) %all-to-all-start.4) | async-done | bytes 2097184 | tf_op jit(solution)/shard_map/all_to_all | solution.py:26
  672.3 6.9 %psum.7 = f32[1,16]{1,0:T(1,128)S(1)} all-reduce(f32[1,16]{1,0:T(1,128)S(1)} %bitcast.147), channel_id=1, replica_groups=mesh['dp'=8,'pipe'=4,'tensor'=4] {'tensor'}, use_global_device_ids=true, to_apply=%region_13.14 | all-reduce | flops 16 | bytes 128 | tf_op jit(solution)/shard_map/psum | solution.py:211
  (326 shorter events, 156.3 us)
Async XLA Ops:
  97.6 6.8 copy-start.5
  97.6 8.1 %copy-start.4 = (s32[2]{0:T(128)S(1)}, s32[2]{0:T(128)}, u32[]{:S(2)}) copy-start(s32[2]{0:T(128)} %param.16) | copy-start | bytes 28
  97.6 88.0 %copy-start = (bf16[1,4096,256]{2,1,0:T(8,128)(2,1)S(1)}, bf16[1,4096,256]{2,1,0:T(8,128)(2,1)}, u32[]{:S(2)}) copy-start(bf16[1,4096,256]{2,1,0:T(8,128)(2,1)} %param.25) | copy-start | bytes 6291460
  97.6 99.5 %all-to-all-start.2 = ((bf16[32,96,1024]{2,1,0:T(8,128)(2,1)}), bf16[32,96,1024]{2,1,0:T(8,128)(2,1)}, u32[]{:S(2)}, u32[]{:S(2)}) async-start(bf16[32,96,1024]{2,1,0:T(8,128)(2,1)} %select_select_fusion), calls=%async_computation.2 | async-start | bytes 12582912 | tf_op jit(solution)/shard_map/all_to_all | solution.py:117
  197.1 4.3 copy-start.1
  201.4 386.9 %copy-start.3 = (s32[2,1]{0,1:T(1,128)S(1)}, s32[2,1]{0,1:T(1,128)}, u32[]{:S(2)}) copy-start(s32[2,1]{0,1:T(1,128)} %param.17) | copy-start | bytes 28
  202.5 16.1 %all-to-all-start = ((bf16[4,96,1024]{2,1,0:T(8,128)(2,1)}), bf16[4,96,1024]{2,1,0:T(8,128)(2,1)S(1)}, u32[]{:S(2)}, u32[]{:S(2)}) async-start(bf16[4,96,1024]{2,1,0:T(8,128)(2,1)} %broadcast_in_dim.169), calls=%async_computation | async-start | bytes 1572864 | tf_op jit(solution)/shard_map/while/body/eval_jaxpr/all_to_all | solution.py:26
  234.0 13.3 %all-to-all-start.1 = ((bf16[4,96,1024]{2,1,0:T(8,128)(2,1)}), bf16[4,96,1024]{2,1,0:T(8,128)(2,1)S(1)}, u32[]{:S(2)}, u32[]{:S(2)}) async-start(bf16[4,96,1024]{2,1,0:T(8,128)(2,1)} %bitcast.122), calls=%async_computation.1 | async-start | bytes 1572864 | tf_op jit(solution)/shard_map/while/body/eval_jaxpr/all_to_all | solution.py:41
  247.5 5.8 collective-permute-start
  254.3 11.8 %all-to-all-start = ((bf16[4,96,1024]{2,1,0:T(8,128)(2,1)}), bf16[4,96,1024]{2,1,0:T(8,128)(2,1)S(1)}, u32[]{:S(2)}, u32[]{:S(2)}) async-start(bf16[4,96,1024]{2,1,0:T(8,128)(2,1)} %broadcast_in_dim.169), calls=%async_computation | async-start | bytes 1572864 | tf_op jit(solution)/shard_map/while/body/eval_jaxpr/all_to_all | solution.py:26
  281.5 11.8 %all-to-all-start.1 = ((bf16[4,96,1024]{2,1,0:T(8,128)(2,1)}), bf16[4,96,1024]{2,1,0:T(8,128)(2,1)S(1)}, u32[]{:S(2)}, u32[]{:S(2)}) async-start(bf16[4,96,1024]{2,1,0:T(8,128)(2,1)} %bitcast.122), calls=%async_computation.1 | async-start | bytes 1572864 | tf_op jit(solution)/shard_map/while/body/eval_jaxpr/all_to_all | solution.py:41
  293.5 6.1 collective-permute-start
  300.6 11.8 %all-to-all-start = ((bf16[4,96,1024]{2,1,0:T(8,128)(2,1)}), bf16[4,96,1024]{2,1,0:T(8,128)(2,1)S(1)}, u32[]{:S(2)}, u32[]{:S(2)}) async-start(bf16[4,96,1024]{2,1,0:T(8,128)(2,1)} %broadcast_in_dim.169), calls=%async_computation | async-start | bytes 1572864 | tf_op jit(solution)/shard_map/while/body/eval_jaxpr/all_to_all | solution.py:26
  327.9 11.8 %all-to-all-start.1 = ((bf16[4,96,1024]{2,1,0:T(8,128)(2,1)}), bf16[4,96,1024]{2,1,0:T(8,128)(2,1)S(1)}, u32[]{:S(2)}, u32[]{:S(2)}) async-start(bf16[4,96,1024]{2,1,0:T(8,128)(2,1)} %bitcast.122), calls=%async_computation.1 | async-start | bytes 1572864 | tf_op jit(solution)/shard_map/while/body/eval_jaxpr/all_to_all | solution.py:41
  339.9 6.1 collective-permute-start
  347.0 11.8 %all-to-all-start = ((bf16[4,96,1024]{2,1,0:T(8,128)(2,1)}), bf16[4,96,1024]{2,1,0:T(8,128)(2,1)S(1)}, u32[]{:S(2)}, u32[]{:S(2)}) async-start(bf16[4,96,1024]{2,1,0:T(8,128)(2,1)} %broadcast_in_dim.169), calls=%async_computation | async-start | bytes 1572864 | tf_op jit(solution)/shard_map/while/body/eval_jaxpr/all_to_all | solution.py:26
  374.2 11.8 %all-to-all-start.1 = ((bf16[4,96,1024]{2,1,0:T(8,128)(2,1)}), bf16[4,96,1024]{2,1,0:T(8,128)(2,1)S(1)}, u32[]{:S(2)}, u32[]{:S(2)}) async-start(bf16[4,96,1024]{2,1,0:T(8,128)(2,1)} %bitcast.122), calls=%async_computation.1 | async-start | bytes 1572864 | tf_op jit(solution)/shard_map/while/body/eval_jaxpr/all_to_all | solution.py:41
  386.2 5.8 collective-permute-start
  393.0 11.8 %all-to-all-start = ((bf16[4,96,1024]{2,1,0:T(8,128)(2,1)}), bf16[4,96,1024]{2,1,0:T(8,128)(2,1)S(1)}, u32[]{:S(2)}, u32[]{:S(2)}) async-start(bf16[4,96,1024]{2,1,0:T(8,128)(2,1)} %broadcast_in_dim.169), calls=%async_computation | async-start | bytes 1572864 | tf_op jit(solution)/shard_map/while/body/eval_jaxpr/all_to_all | solution.py:26
  420.2 11.8 %all-to-all-start.1 = ((bf16[4,96,1024]{2,1,0:T(8,128)(2,1)}), bf16[4,96,1024]{2,1,0:T(8,128)(2,1)S(1)}, u32[]{:S(2)}, u32[]{:S(2)}) async-start(bf16[4,96,1024]{2,1,0:T(8,128)(2,1)} %bitcast.122), calls=%async_computation.1 | async-start | bytes 1572864 | tf_op jit(solution)/shard_map/while/body/eval_jaxpr/all_to_all | solution.py:41
  432.2 5.8 collective-permute-start
  439.1 13.1 %all-to-all-start = ((bf16[4,96,1024]{2,1,0:T(8,128)(2,1)}), bf16[4,96,1024]{2,1,0:T(8,128)(2,1)S(1)}, u32[]{:S(2)}, u32[]{:S(2)}) async-start(bf16[4,96,1024]{2,1,0:T(8,128)(2,1)} %broadcast_in_dim.169), calls=%async_computation | async-start | bytes 1572864 | tf_op jit(solution)/shard_map/while/body/eval_jaxpr/all_to_all | solution.py:26
  467.6 11.8 %all-to-all-start.1 = ((bf16[4,96,1024]{2,1,0:T(8,128)(2,1)}), bf16[4,96,1024]{2,1,0:T(8,128)(2,1)S(1)}, u32[]{:S(2)}, u32[]{:S(2)}) async-start(bf16[4,96,1024]{2,1,0:T(8,128)(2,1)} %bitcast.122), calls=%async_computation.1 | async-start | bytes 1572864 | tf_op jit(solution)/shard_map/while/body/eval_jaxpr/all_to_all | solution.py:41
  479.6 5.8 collective-permute-start
  486.4 15.8 %all-to-all-start = ((bf16[4,96,1024]{2,1,0:T(8,128)(2,1)}), bf16[4,96,1024]{2,1,0:T(8,128)(2,1)S(1)}, u32[]{:S(2)}, u32[]{:S(2)}) async-start(bf16[4,96,1024]{2,1,0:T(8,128)(2,1)} %broadcast_in_dim.169), calls=%async_computation | async-start | bytes 1572864 | tf_op jit(solution)/shard_map/while/body/eval_jaxpr/all_to_all | solution.py:26
  517.6 11.8 %all-to-all-start.1 = ((bf16[4,96,1024]{2,1,0:T(8,128)(2,1)}), bf16[4,96,1024]{2,1,0:T(8,128)(2,1)S(1)}, u32[]{:S(2)}, u32[]{:S(2)}) async-start(bf16[4,96,1024]{2,1,0:T(8,128)(2,1)} %bitcast.122), calls=%async_computation.1 | async-start | bytes 1572864 | tf_op jit(solution)/shard_map/while/body/eval_jaxpr/all_to_all | solution.py:41
  529.6 5.8 collective-permute-start
  536.4 12.3 %all-to-all-start = ((bf16[4,96,1024]{2,1,0:T(8,128)(2,1)}), bf16[4,96,1024]{2,1,0:T(8,128)(2,1)S(1)}, u32[]{:S(2)}, u32[]{:S(2)}) async-start(bf16[4,96,1024]{2,1,0:T(8,128)(2,1)} %broadcast_in_dim.169), calls=%async_computation | async-start | bytes 1572864 | tf_op jit(solution)/shard_map/while/body/eval_jaxpr/all_to_all | solution.py:26
  564.2 13.6 %all-to-all-start.1 = ((bf16[4,96,1024]{2,1,0:T(8,128)(2,1)}), bf16[4,96,1024]{2,1,0:T(8,128)(2,1)S(1)}, u32[]{:S(2)}, u32[]{:S(2)}) async-start(bf16[4,96,1024]{2,1,0:T(8,128)(2,1)} %bitcast.122), calls=%async_computation.1 | async-start | bytes 1572864 | tf_op jit(solution)/shard_map/while/body/eval_jaxpr/all_to_all | solution.py:41
  577.9 5.8 collective-permute-start
  584.7 11.8 %all-to-all-start.3 = ((bf16[4,96,1024]{2,1,0:T(8,128)(2,1)}), bf16[4,96,1024]{2,1,0:T(8,128)(2,1)S(1)}, u32[]{:S(2)}, u32[]{:S(2)}) async-start(bf16[4,96,1024]{2,1,0:T(8,128)(2,1)} %broadcast_in_dim.128), calls=%async_computation.3 | async-start | bytes 1572864 | tf_op jit(solution)/shard_map/all_to_all | solution.py:26
  588.2 43.7 %dynamic-slice-start = ((f32[4096]{0:T(1024)}, s32[]{:T(128)}), f32[1024]{0:T(1024)S(1)}, s32[]{:S(2)}) async-start(f32[4096]{0:T(1024)} %param.27, s32[]{:T(128)} %select_n.118), calls=%async_computation.6 | async-start | bytes 8704 | tf_op jit(solution)/shard_map/dynamic_slice | solution.py:183
  597.1 41.1 %all-to-all-start.5 = ((bf16[32,1,32]{2,1,0:T(2,128)(2,1)}), bf16[32,1,32]{2,1,0:T(2,128)(2,1)S(1)}, u32[]{:S(2)}, u32[]{:S(2)}) async-start(bf16[32,1,32]{2,1,0:T(2,128)(2,1)} %broadcast_in_dim.130), calls=%async_computation.5 | async-start | bytes 32768 | tf_op jit(solution)/shard_map/all_to_all | solution.py:26
  639.8 31.5 %all-to-all-start.4 = ((bf16[32,32,1024]{2,1,0:T(8,128)(2,1)}), bf16[32,32,1024]{2,1,0:T(8,128)(2,1)S(1)}, u32[]{:S(2)}, u32[]{:S(2)}) async-start(bf16[32,32,1024]{2,1,0:T(8,128)(2,1)} %broadcast_in_dim.129), calls=%async_computation.4 | async-start | bytes 4194304 | tf_op jit(solution)/shard_map/all_to_all | solution.py:26
  671.7 8.0 %copy-start.2 = (f32[32,1024]{1,0:T(8,128)}, f32[32,1024]{1,0:T(8,128)S(1)}, u32[]{:S(2)}) copy-start(f32[32,1024]{1,0:T(8,128)S(1)} %broadcast_divide_fusion) | copy-start | bytes 393220
where the time goes:
time: 684 us; the launch traced here: 680 us
  waiting for transfers between devices  216 us (32%)
  blocking collectives  157 us (23%)
  starting transfers between devices  107 us (16%)
  matrix products  104 us (15%)
  local copies, waits for them, and re-layouts  51.8 us (8%)
  other arithmetic  39.9 us (6%)
    all_to_all x11, waiting for transfers between devices, sent_to_all(): return lax.all_to_all(copies, axis, split_axis=0, concat_axis=0, tiled=True)  101 us
    unnamed x1, blocking collectives  78.8 us
    all_to_all x11, starting transfers between devices, sent_to_all(): return lax.all_to_all(copies, axis, split_axis=0, concat_axis=0, tiled=True)  71.5 us
    all_to_all x8, waiting for transfers between devices, sum_at_owner(): lax.all_to_all(split_up(shard, dim, length), axis, 0, 0, tiled=True)  69.5 us
    dot_general x8, matrix products, section_block(): projected = jnp.dot(normed, w_in, preferred_element_type=jnp.float32)  54.2 us
    ppermute x8, waiting for transfers between devices, passed_along(): return lax.ppermute(block, axis, route)  45.3 us
    dot_general x8, matrix products, section_block(): partial_out = jnp.dot(mixed, out_proj, preferred_element_type=jnp.float32)  38.7 us
    all_gather x1, blocking collectives, shards(): lax.all_gather(support_tokens, ('dp', 'pipe'), axis=0, tiled=True)  37 us
  transfers between devices with their start and end apart: 28, of which 27 were waited for; matrix products, arithmetic and copies ran while one was open for 4% of the time, Pallas kernels for 0%

commit v1 on v0

--- a/solution.py
+++ b/solution.py
@@ -1,8 +1,11 @@
+import functools
 import math
 
 import jax
 import jax.numpy as jnp
 from jax import lax
+from jax.experimental import pallas as pl
+from jax.experimental.pallas import tpu as pltpu
 from jax.sharding import PartitionSpec as P
 
 D = 4096
@@ -78,7 +81,7 @@
     return values * lax.rsqrt(mean_square + epsilon) * gain_vector
 
 
-def shards(
+def plain_shards(
     support_tokens,
     support_lengths,
     support_labels,
@@ -213,6 +216,713 @@
     return (prototypes, logits)
 
 
+MESH = pl.DeviceIdType.MESH
+GROUPS = 32
+PIPE = 4
+TENSOR = 4
+LANES = 8
+STEPS = 4
+SLOTS = 64
+CAP = 16
+SHARD = 1024
+HIGH = lax.Precision.HIGHEST
+
+
+def place():
+    return lax.axis_index("dp"), lax.axis_index("pipe"), lax.axis_index("tensor")
+
+
+def peer(dp, pipe, tensor):
+    return {"dp": dp, "pipe": pipe, "tensor": tensor}
+
+
+def greet(with_tensor):
+    dp, pipe, tensor = place()
+    mine = dp * PIPE + pipe
+    barrier = pltpu.get_barrier_semaphore()
+    for step in range(1, GROUPS):
+        other = lax.rem(mine + step, GROUPS)
+        pl.semaphore_signal(
+            barrier,
+            inc=1,
+            device_id=peer(other // PIPE, lax.rem(other, PIPE), tensor),
+            device_id_type=MESH,
+        )
+    count = GROUPS - 1
+    if with_tensor:
+        for step in range(1, TENSOR):
+            pl.semaphore_signal(
+                barrier,
+                inc=1,
+                device_id=peer(dp, pipe, lax.rem(tensor + step, TENSOR)),
+                device_id_type=MESH,
+            )
+        count += TENSOR - 1
+    pl.semaphore_wait(barrier, count)
+
+
+def remote(src, dst, send_sem, recv_sem, device):
+    return pltpu.make_async_remote_copy(
+        src_ref=src,
+        dst_ref=dst,
+        send_sem=send_sem,
+        recv_sem=recv_sem,
+        device_id=device,
+        device_id_type=MESH,
+    )
+
+
+def ids_kernel(row_ref, out_ref, held, send_sem, recv_sem):
+    dp, pipe, tensor = place()
+    mine = dp * PIPE + pipe
+    greet(False)
+    copies = []
+    for step in range(1, GROUPS):
+        other = lax.rem(mine + step, GROUPS)
+        copy = remote(
+            row_ref,
+            held.at[mine],
+            send_sem.at[step],
+            recv_sem.at[step],
+            peer(other // PIPE, lax.rem(other, PIPE), tensor),
+        )
+        copy.start()
+        copies.append(copy)
+    held[mine] = row_ref[...]
+    for step in range(1, GROUPS):
+        source = lax.rem(mine - step + GROUPS, GROUPS)
+        remote(
+            row_ref, held.at[source], send_sem.at[step], recv_sem.at[step], peer(dp, pipe, tensor)
+        ).wait_recv()
+    out_ref[...] = held[...]
+    for copy in copies:
+        copy.wait_send()
+
+
+def share_ids(row):
+    return pl.pallas_call(
+        ids_kernel,
+        out_shape=jax.ShapeDtypeStruct((GROUPS, 1, 128), jnp.int32),
+        in_specs=[pl.BlockSpec(memory_space=pltpu.VMEM)],
+        out_specs=pl.BlockSpec(memory_space=pltpu.VMEM),
+        scratch_shapes=[
+            pltpu.VMEM((GROUPS, 1, 128), jnp.int32),
+            pltpu.SemaphoreType.DMA((GROUPS,)),
+            pltpu.SemaphoreType.DMA((GROUPS,)),
+        ],
+        compiler_params=pltpu.CompilerParams(collective_id=0, has_side_effects=True),
+        name="share_ids",
+    )(row).reshape(GROUPS, 128)
+
+
+def trunk_kernel(
+    rows_ref,
+    slot_ref,
+    cos_ref,
+    sin_ref,
+    bias_ref,
+    gain_ref,
+    wq_ref,
+    wk_ref,
+    wv_ref,
+    wo_ref,
+    out_ref,
+    w_in,
+    w_out,
+    emb,
+    ag,
+    rs,
+    po,
+    moved,
+    nbuf,
+    mix,
+    w_sem,
+    emb_send,
+    emb_recv,
+    ag_send,
+    ag_recv,
+    rs_send,
+    rs_recv,
+    mv_send,
+    mv_recv,
+):
+    dp, pipe, tensor = place()
+    mine = dp * PIPE + pipe
+    loads = [
+        pltpu.make_async_copy(wq_ref.at[0], w_in.at[:, pl.ds(0, 1024)], w_sem.at[0]),
+        pltpu.make_async_copy(wk_ref.at[0], w_in.at[:, pl.ds(1024, 256)], w_sem.at[1]),
+        pltpu.make_async_copy(wv_ref.at[0], w_in.at[:, pl.ds(1280, 256)], w_sem.at[2]),
+    ] + [
+        pltpu.make_async_copy(
+            wo_ref.at[0, :, pl.ds(i * SHARD, SHARD)], w_out.at[i], w_sem.at[3 + i]
+        )
+        for i in range(TENSOR)
+    ]
+    for load in loads:
+        load.start()
+    greet(True)
+
+    def emb_copy(lane):
+        return remote(
+            rows_ref.at[lane],
+            emb.at[mine],
+            emb_send.at[lane],
+            emb_recv.at[mine],
+            peer(lane, 0, tensor),
+        )
+
+    for lane in range(LANES):
+
+        @pl.when(mine != lane * PIPE)
+        def _():
+            emb_copy(lane).start()
+
+    @pl.when(pipe == 0)
+    def _():
+        emb[mine] = rows_ref[dp]
+
+        def wait_source(source, carry):
+            @pl.when(source != mine)
+            def _():
+                remote(
+                    rows_ref.at[0],
+                    emb.at[source],
+                    emb_send.at[0],
+                    emb_recv.at[source],
+                    peer(dp, pipe, tensor),
+                ).wait_recv()
+
+            return carry
+
+        lax.fori_loop(0, GROUPS, wait_source, 0)
+
+    for load in loads:
+        load.wait()
+
+    def ag_copy(step, j):
+        other = lax.rem(tensor + j, TENSOR)
+        return remote(
+            ag.at[step, tensor],
+            ag.at[step, tensor],
+            ag_send.at[step, j],
+            ag_recv.at[step, j],
+            peer(dp, pipe, other),
+        )
+
+    def rs_copy(step, j):
+        other = lax.rem(tensor + j, TENSOR)
+        return remote(
+            po.at[step, other],
+            rs.at[step, tensor],
+            rs_send.at[step, j],
+            rs_recv.at[step, j],
+            peer(dp, pipe, other),
+        )
+
+    def mv_copy(step):
+        return remote(
+            moved.at[step],
+            ag.at[step, tensor],
+            mv_send.at[step],
+            mv_recv.at[step],
+            peer(dp, lax.rem(pipe + 1, PIPE), tensor),
+        )
+
+    def take(step):
+        @pl.when(pipe == 0)
+        def _():
+            pick = lax.broadcasted_iota(jnp.int32, (SLOTS, GROUPS * CAP), 1)
+            onehot = (pick == slot_ref[step]).astype(jnp.float32).astype(jnp.bfloat16)
+            table = emb[...].reshape(GROUPS * CAP, SHARD)
+            ag[step, tensor] = jnp.dot(
+                onehot, table, preferred_element_type=jnp.float32
+            ).astype(jnp.bfloat16)
+
+        @pl.when(pipe > 0)
+        def _():
+            mv_copy(step).wait_recv()
+
+        for j in (2, 1, 3):
+            ag_copy(step, j).start()
+
+    def compute(step):
+        for j in (1, 3, 2):
+            source = lax.rem(tensor - j + TENSOR, TENSOR)
+            remote(
+                ag.at[step, source],
+                ag.at[step, source],
+                ag_send.at[step, j],
+                ag_recv.at[step, j],
+                peer(dp, pipe, tensor),
+            ).wait_recv()
+        total = jnp.zeros((SLOTS, 1), jnp.float32)
+        for s in range(TENSOR):
+            values = ag[step, s].astype(jnp.float32)
+            total += jnp.sum(values * values, axis=-1, keepdims=True)
+        factor = lax.rsqrt(total / D + epsilon)
+        for s in range(TENSOR):
+            values = ag[step, s].astype(jnp.float32)
+            cols = slice(s * SHARD, (s + 1) * SHARD)
+            nbuf[:, cols] = (values * factor * gain_ref[:, cols]).astype(jnp.bfloat16)
+        cosine = cos_ref[step]
+        sine = sin_ref[step]
+        bias = bias_ref[step]
+        bias4 = jnp.concatenate([bias] * 4, axis=0)
+        scale = 1.0 / math.sqrt(HEAD_DIM)
+
+        def turned(block):
+            return (block * cosine + pltpu.roll(block, 64, 1) * sine).astype(jnp.bfloat16)
+
+        normed = nbuf[...]
+        kv = jnp.dot(normed, w_in[:, 1024:1536], preferred_element_type=jnp.float32)
+        for g in range(2):
+            qs = jnp.dot(
+                normed, w_in[:, g * 512 : (g + 1) * 512], preferred_element_type=jnp.float32
+            )
+            key = turned(kv[:, g * 128 : (g + 1) * 128])
+            value = kv[:, 256 + g * 128 : 256 + (g + 1) * 128].astype(jnp.bfloat16)
+            query = jnp.concatenate(
+                [turned(qs[:, h * 128 : (h + 1) * 128]) for h in range(4)], axis=0
+            )
+            scores = lax.dot_general(
+                query, key, (((1,), (1,)), ((), ())), preferred_element_type=jnp.float32
+            )
+            scores = scores * scale + bias4
+            top = jnp.max(scores, axis=-1, keepdims=True)
+            raised = jnp.exp(scores - top)
+            weights = (raised / jnp.sum(raised, axis=-1, keepdims=True)).astype(jnp.bfloat16)
+            mixed = jnp.dot(weights, value, preferred_element_type=jnp.float32)
+            mixed = mixed.astype(jnp.bfloat16)
+            for h in range(4):
+                cols = slice(g * 512 + h * 128, g * 512 + (h + 1) * 128)
+                mix[:, cols] = mixed[h * SLOTS : (h + 1) * SLOTS]
+        for j in (2, 1, 3, 0):
+            other = lax.rem(tensor + j, TENSOR)
+            part = jnp.dot(mix[...], w_out[other], preferred_element_type=jnp.float32)
+            po[step, other] = part.astype(jnp.bfloat16)
+            if j:
+                rs_copy(step, j).start()
+
+    def settle(step):
+        total = po[step, tensor].astype(jnp.float32)
+        for j in (1, 3, 2):
+            source = lax.rem(tensor - j + TENSOR, TENSOR)
+            remote(
+                po.at[step, 0],
+                rs.at[step, source],
+                rs_send.at[step, j],
+                rs_recv.at[step, j],
+                peer(dp, pipe, tensor),
+            ).wait_recv()
+            total += rs[step, source].astype(jnp.float32)
+        moved[step] = (ag[step, tensor].astype(jnp.float32) + total).astype(jnp.bfloat16)
+
+        @pl.when(pipe < PIPE - 1)
+        def _():
+            mv_copy(step).start()
+
+    take(0)
+
+    def body(step, carry):
+        compute(step)
+
+        @pl.when(step < STEPS - 1)
+        def _():
+            take(lax.min(step + 1, STEPS - 1))
+
+        settle(step)
+        return carry
+
+    lax.fori_loop(0, STEPS, body, 0)
+    out_ref[...] = moved[...]
+
+    def drain(step, carry):
+        for j in (1, 2, 3):
+            ag_copy(step, j).wait_send()
+            rs_copy(step, j).wait_send()
+
+        @pl.when(pipe < PIPE - 1)
+        def _():
+            mv_copy(step).wait_send()
+
+        return carry
+
+    lax.fori_loop(0, STEPS, drain, 0)
+    for lane in range(LANES):
+
+        @pl.when(mine != lane * PIPE)
+        def _():
+            emb_copy(lane).wait_send()
+
+
+def trunk(rows, slots, cosine, sine, bias, gain, wq, wk, wv, wo):
+    vmem = pl.BlockSpec(memory_space=pltpu.VMEM)
+    hbm = pl.BlockSpec(memory_space=pl.ANY)
+    sems = pltpu.SemaphoreType.DMA
+    return pl.pallas_call(
+        trunk_kernel,
+        out_shape=jax.ShapeDtypeStruct((STEPS, SLOTS, SHARD), jnp.bfloat16),
+        in_specs=[vmem] * 6 + [hbm] * 4,
+        out_specs=vmem,
+        scratch_shapes=[
+            pltpu.VMEM((D, 1536), jnp.bfloat16),
+            pltpu.VMEM((TENSOR, SHARD, SHARD), jnp.bfloat16),
+            pltpu.VMEM((GROUPS, CAP, SHARD), jnp.bfloat16),
+            pltpu.VMEM((STEPS, TENSOR, SLOTS, SHARD), jnp.bfloat16),
+            pltpu.VMEM((STEPS, TENSOR, SLOTS, SHARD), jnp.bfloat16),
+            pltpu.VMEM((STEPS, TENSOR, SLOTS, SHARD), jnp.bfloat16),
+            pltpu.VMEM((STEPS, SLOTS, SHARD), jnp.bfloat16),
+            pltpu.VMEM((SLOTS, D), jnp.bfloat16),
+            pltpu.VMEM((SLOTS, SHARD), jnp.bfloat16),
+            sems((7,)),
+            sems((LANES,)),
+            sems((GROUPS,)),
+            sems((STEPS, TENSOR)),
+            sems((STEPS, TENSOR)),
+            sems((STEPS, TENSOR)),
+            sems((STEPS, TENSOR)),
+            sems((STEPS,)),
+            sems((STEPS,)),
+        ],
+        compiler_params=pltpu.CompilerParams(
+            collective_id=1, has_side_effects=True, vmem_limit_bytes=52 * 1024 * 1024
+        ),
+        name="trunk",
+    )(rows, slots, cosine, sine, bias, gain, wq, wk, wv, wo)
+
+
+def close_kernel(
+    hid_ref,
+    weight_ref,
+    gain_ref,
+    count_ref,
+    episode_ref,
+    proto_ref,
+    logit_ref,
+    part,
+    parts,
+    sq,
+    sqs,
+    done,
+    dones,
+    dist,
+    dists,
+    sq_send,
+    sq_recv,
+    part_send,
+    part_recv,
+    done_send,
+    done_recv,
+    dist_send,
+    dist_recv,
+):
+    dp, pipe, tensor = place()
+    mine = dp * PIPE + pipe
+    last = PIPE - 1
+    tokens = STEPS * SLOTS
+    greet(True)
+
+    def sq_copy(j):
+        other = lax.rem(tensor + j, TENSOR)
+        return remote(sq, sqs.at[j], sq_send.at[j], sq_recv.at[j], peer(dp, pipe, other))
+
+    def part_copy(j):
+        other = lax.rem(dp + j, LANES)
+        return remote(
+            part.at[other], parts.at[j], part_send.at[j], part_recv.at[j], peer(other, pipe, tensor)
+        )
+
+    def done_copy(step):
+        other = lax.rem(mine + step, GROUPS)
+        return remote(
+            done,
+            dones.at[dp],
+            done_send.at[step],
+            done_recv.at[dp],
+            peer(other // PIPE, lax.rem(other, PIPE), tensor),
+        )
+
+    def dist_copy(j):
+        other = lax.rem(tensor + j, TENSOR)
+        return remote(
+            dist, dists.at[j], dist_send.at[j], dist_recv.at[j], peer(dp, pipe, other)
+        )
+
+    @pl.when(pipe == last)
+    def _():
+        values = hid_ref[...].astype(jnp.float32).reshape(tokens, SHARD)
+        ones = jnp.ones((8, SHARD), jnp.float32)
+        sq[...] = lax.dot_general(
+            ones,
+            values * values,
+            (((1,), (1,)), ((), ())),
+            precision=HIGH,
+            preferred_element_type=jnp.float32,
+        )
+        for j in (2, 1, 3):
+            sq_copy(j).start()
+        total = sq[...]
+        for j in (1, 3, 2):
+            sq_copy(j).wait_recv()
+            total += sqs[j]
+        factor = lax.rsqrt(total[0:1] / D + epsilon)
+        pooled = jnp.dot(
+            weight_ref[...] * factor, values, precision=HIGH, preferred_element_type=jnp.float32
+        )
+        part[...] = (pooled * gain_ref[...]).reshape(LANES, 8, SHARD)
+        for j in range(1, LANES):
+            part_copy(j).start()
+        whole = part[dp]
+        for j in range(1, LANES):
+            part_copy(j).wait_recv()
+            whole += parts[j]
+        done[...] = whole / count_ref[...]
+        for step in range(1, GROUPS):
+            done_copy(step).start()
+        dones[dp] = done[...]
+
+    for lane in range(LANES):
+
+        @pl.when(mine != lane * PIPE + last)
+        def _():
+            remote(
+                done, dones.at[lane], done_send.at[0], done_recv.at[lane], peer(dp, pipe, tensor)
+            ).wait_recv()
+
+    for lane in range(LANES):
+        proto_ref[lane * 4 : (lane + 1) * 4, :] = dones[lane, 0:4, :]
+    query = dones[dp, pl.ds(4 + pipe, 1), :]
+    gap = proto_ref[...] - query
+    dist[...] = lax.dot_general(
+        jnp.ones((8, SHARD), jnp.float32),
+        gap * gap,
+        (((1,), (1,)), ((), ())),
+        precision=HIGH,
+        preferred_element_type=jnp.float32,
+    )
+    for j in (2, 1, 3):
+        dist_copy(j).start()
+    total = dist[...]
+    for j in (1, 3, 2):
+        dist_copy(j).wait_recv()
+        total += dists[j]
+    scaled = total[0:1] * (-1.0 / math.sqrt(D))
+    logit_ref[...] = jnp.where(episode_ref[...] == 0, scaled[:, 0:WAYS], scaled[:, WAYS:])
+
+    for j in (1, 2, 3):
+        dist_copy(j).wait_send()
+
+    @pl.when(pipe == last)
+    def _():
+        for j in (1, 2, 3):
+            sq_copy(j).wait_send()
+        for j in range(1, LANES):
+            part_copy(j).wait_send()
+        for step in range(1, GROUPS):
+            done_copy(step).wait_send()
+
+
+def close(hidden, weight, gain, count, episode):
+    vmem = pl.BlockSpec(memory_space=pltpu.VMEM)
+    sems = pltpu.SemaphoreType.DMA
+    f32 = jnp.float32
+    tokens = STEPS * SLOTS
+    return pl.pallas_call(
+        close_kernel,
+        out_shape=(
+            jax.ShapeDtypeStruct((EPISODES * WAYS, SHARD), f32),
+            jax.ShapeDtypeStruct((1, WAYS), f32),
+        ),
+        in_specs=[vmem] * 5,
+        out_specs=(vmem, vmem),
+        scratch_shapes=[
+            pltpu.VMEM((LANES, 8, SHARD), f32),
+            pltpu.VMEM((LANES, 8, SHARD), f32),
+            pltpu.VMEM((8, tokens), f32),
+            pltpu.VMEM((TENSOR, 8, tokens), f32),
+            pltpu.VMEM((8, SHARD), f32),
+            pltpu.VMEM((LANES, 8, SHARD), f32),
+            pltpu.VMEM((8, EPISODES * WAYS), f32),
+            pltpu.VMEM((TENSOR, 8, EPISODES * WAYS), f32),
+            sems((TENSOR,)),
+            sems((TENSOR,)),
+            sems((LANES,)),
+            sems((LANES,)),
+            sems((GROUPS,)),
+            sems((LANES,)),
+            sems((TENSOR,)),
+            sems((TENSOR,)),
+        ],
+        compiler_params=pltpu.CompilerParams(collective_id=2, has_side_effects=True),
+        name="close",
+    )(hidden, weight, gain, count, episode)
+
+
+def own(table, index):
+    return lax.dynamic_index_in_dim(table, index, 0, keepdims=False)
+
+
+def shards(
+    support_tokens,
+    support_lengths,
+    support_labels,
+    query_tokens,
+    query_lengths,
+    query_episodes,
+    embedding,
+    attn_gain,
+    query_weight,
+    key_weight,
+    value_weight,
+    out_weight,
+    final_gain,
+):
+    dp, pipe, tensor = place()
+    mine = dp * PIPE + pipe
+    table_rows = embedding.shape[0]
+    row = jnp.concatenate(
+        [
+            support_tokens.reshape(64),
+            query_tokens.reshape(32),
+            support_lengths,
+            query_lengths,
+            support_labels.reshape(2),
+            jnp.zeros((27,), jnp.int32),
+        ]
+    ).reshape(1, 128)
+    every = share_ids(row)
+    tokens = every[:, :96].reshape(96, 32)
+    lengths = every[:, 96:99].reshape(96)
+    labels = every[:, 99:101]
+    group = jnp.arange(GROUPS)
+    class_row = (labels // 4) * 8 + labels % 4
+    query_row = (group // 4) * 8 + 4 + group % 4
+    target = jnp.concatenate([class_row, query_row[:, None]], axis=1).reshape(96)
+
+    index = jnp.arange(96)
+    ahead = (lengths[None, :] > lengths[:, None]) | (
+        (lengths[None, :] == lengths[:, None]) & (index[None, :] < index[:, None])
+    )
+    rank = jnp.sum(ahead.astype(jnp.int32), axis=1)
+    at_rank = rank[None, :] == index[:, None]
+    seq_of = jnp.sum(jnp.where(at_rank, index[None, :], 0), axis=1)
+    len_of = jnp.sum(jnp.where(at_rank, lengths[None, :], 0), axis=1)
+    bins = LANES * STEPS
+    first_two = len_of[:bins] + len_of[bins : 2 * bins][::-1]
+    bin_id = jnp.arange(bins)
+    below = (first_two[None, :] < first_two[:, None]) | (
+        (first_two[None, :] == first_two[:, None]) & (bin_id[None, :] < bin_id[:, None])
+    )
+    third = jnp.sum(below.astype(jnp.int32), axis=1)
+    at_third = third[:, None] == bin_id[None, :]
+    seq_third = jnp.sum(jnp.where(at_third, seq_of[None, 2 * bins :], 0), axis=1)
+    len_third = jnp.sum(jnp.where(at_third, len_of[None, 2 * bins :], 0), axis=1)
+    len_a, len_b, len_c = len_of[:bins], len_of[bins : 2 * bins][::-1], len_third
+    seq_a, seq_b, seq_c = seq_of[:bins], seq_of[bins : 2 * bins][::-1], seq_third
+    full = len_a + len_b + len_c
+    slot = jnp.arange(SLOTS)[None, :]
+    in_a = slot < len_a[:, None]
+    in_b = slot < (len_a + len_b)[:, None]
+    live = slot < full[:, None]
+    seq = jnp.where(in_a, seq_a[:, None], jnp.where(in_b, seq_b[:, None], seq_c[:, None]))
+    position = slot - jnp.where(
+        in_a, 0, jnp.where(in_b, len_a[:, None], (len_a + len_b)[:, None])
+    )
+    seq_hot = (seq[:, :, None] == index[None, None, :]).astype(jnp.float32)
+    facts = jnp.concatenate([tokens, lengths[:, None], target[:, None]], axis=1)
+    slot_facts = jnp.dot(
+        seq_hot.reshape(bins * SLOTS, 96), facts.astype(jnp.float32), precision=HIGH
+    ).astype(jnp.int32)
+    at_position = position.reshape(-1, 1) == jnp.arange(32)[None, :]
+    token = jnp.sum(jnp.where(at_position, slot_facts[:, :32], 0), axis=1)
+
+    count = STEPS * SLOTS
+    token = token.reshape(LANES, count)
+    live = live.reshape(LANES, count)
+    holder = jnp.where(live, token // table_rows, GROUPS)
+    local = token - holder * table_rows
+    order = jnp.arange(count)
+    same = (token[:, None, :] == token[:, :, None]) & live[:, None, :]
+    repeated = jnp.any(same & (order[None, None, :] < order[None, :, None]), axis=2)
+    leads = live & ~repeated
+    before = (
+        leads[:, None, :]
+        & (holder[:, None, :] == holder[:, :, None])
+        & (token[:, None, :] < token[:, :, None])
+    )
+    place_in = jnp.sum(before.astype(jnp.int32), axis=2)
+    fits = jnp.all(full <= SLOTS) & jnp.all(jnp.where(live, place_in, 0) < CAP)
+    wanted = (leads & (holder == mine))[:, None, :] & (
+        place_in[:, None, :] == jnp.arange(CAP)[None, :, None]
+    )
+    picked = jnp.sum(jnp.where(wanted, local[:, None, :], 0), axis=2)
+
+    my_live = own(live, dp)
+    my_slots = jnp.where(my_live, own(holder, dp) * CAP + own(place_in, dp), -1)
+    my_seq = own(seq.reshape(LANES, STEPS, SLOTS), dp)
+    my_pos = own(position.reshape(LANES, STEPS, SLOTS), dp)
+    my_facts = own(slot_facts.reshape(LANES, count, 34), dp)
+    seen = (
+        (my_seq[:, :, None] == my_seq[:, None, :])
+        & (my_pos[:, None, :] <= my_pos[:, :, None])
+        & my_live.reshape(STEPS, 1, SLOTS)
+    )
+    bias = jnp.where(seen, 0.0, -1e30).astype(jnp.float32)
+    half = HEAD_DIM // 2
+    freqs = jnp.exp(
+        -math.log(rotary_base) * jnp.arange(half, dtype=jnp.float32) * (2.0 / HEAD_DIM)
+    )
+    angles = my_pos.astype(jnp.float32)[:, :, None] * freqs
+    cosine, sine = jnp.cos(angles), jnp.sin(angles)
+    cosine = jnp.concatenate([cosine, cosine], axis=-1)
+    sine = jnp.concatenate([-sine, sine], axis=-1)
+    weight = jnp.where(
+        my_live[None, :] & (my_facts[:, 33][None, :] == jnp.arange(64)[:, None]),
+        1.0 / my_facts[:, 32].astype(jnp.float32)[None, :],
+        0.0,
+    )
+    own_class = dp * 4 + jnp.arange(4)
+    class_count = jnp.sum(
+        (labels.reshape(1, 64) == own_class[:, None]).astype(jnp.float32), axis=1
+    )
+    class_count = jnp.concatenate([class_count, jnp.ones((4,), jnp.float32)])[:, None]
+    gain = lax.dynamic_slice_in_dim(final_gain, tensor * SHARD, SHARD).reshape(1, SHARD)
+    episode = jnp.broadcast_to(query_episodes[:, None], (1, WAYS))
+    rest = (
+        support_tokens,
+        support_lengths,
+        support_labels,
+        query_tokens,
+        query_lengths,
+        query_episodes,
+        embedding,
+        attn_gain,
+        query_weight,
+        key_weight,
+        value_weight,
+        out_weight,
+        final_gain,
+    )
+
+    def packed(_):
+        rows = jnp.take(embedding, picked.reshape(-1), axis=0).reshape(LANES, CAP, SHARD)
+        hidden = trunk(
+            rows,
+            my_slots.reshape(STEPS, SLOTS, 1),
+            cosine,
+            sine,
+            bias,
+            attn_gain,
+            query_weight,
+            key_weight,
+            value_weight,
+            out_weight,
+        )
+        return close(hidden, weight, gain, class_count, episode)
+
+    return lax.cond(fits, packed, lambda _: plain_shards(*rest), 0)
+
+
 def solution(mesh):
     return jax.shard_map(
         shards,

time: 684 us -> 239 us (0.35)
  waiting for transfers between devices: 216 us -> 0 us
  Pallas kernels: 0 us -> 203 us
  blocking collectives: 157 us -> 0 us
  starting transfers between devices: 107 us -> 0 us
  matrix products: 104 us -> 0.84 us
  local copies, waits for them, and re-layouts: 51.8 us -> 20.1 us
  other arithmetic: 39.9 us -> 11.8 us
    pallas_call x0 -> x3, Pallas kernels: none -> 203 us  [the longest x1 98.4 us: close(): pl.pallas_call(close_kernel, out_shape=(jax.ShapeDtypeStruct((EPISODES *...]
    all_to_all x20 -> x0, waiting for transfers between devices: 170 us -> none  [the longest x11 101 us: sent_to_all(): return lax.all_to_all(copies, axis, split_axis=0, concat_axis=0, tiled=True)]
    all_to_all x20 -> x0, starting transfers between devices: 106 us -> none  [the longest x11 71.5 us: sent_to_all(): return lax.all_to_all(copies, axis, split_axis=0, concat_axis=0, tiled=True)]
    dot_general x26 -> x1, matrix products: 99.5 us -> 0.84 us  [shards(): jnp.dot(seq_hot.reshape(bins * SLOTS, 96), facts.astype(jnp.float32), pre...]
    unnamed x1 -> x0, blocking collectives: 78.8 us -> none
    all_gather x2 -> x0, blocking collectives: 71 us -> none  [the longest x1 37 us: shards(): lax.all_gather(support_tokens, ('dp', 'pipe'), axis=0, tiled=True)]
    ppermute x8 -> x0, waiting for transfers between devices: 45.3 us -> none  [passed_along(): return lax.ppermute(block, axis, route)]
    concatenate x9 -> x3, other arithmetic: 17.5 us -> 1.58 us  [the longest x1 0.76 us: shards(): cosine = jnp.concatenate([cosine, cosine], axis=-1)]
  transfers between devices with their start and end apart: 28 -> 0, of which waited for: 27 -> 0; matrix products, arithmetic and copies ran while one was open for 4% -> 0% of each run, Pallas kernels for 0% -> 0%
where the time goes in v1:
time: 239 us; the launch traced here: 238 us
  Pallas kernels  203 us (85%)
  local copies, waits for them, and re-layouts  20.1 us (8%)
  other arithmetic  11.8 us (5%)
  between operations  2.77 us (1%)
    pallas_call x1, Pallas kernels, close(): pl.pallas_call(close_kernel, out_shape=(jax.ShapeDtypeStruct((EPISODES *...  98.4 us
    pallas_call x1, Pallas kernels, trunk(): pl.pallas_call(trunk_kernel, out_shape=jax.ShapeDtypeStruct((STEPS, SLOTS...  92.2 us
    pallas_call x1, Pallas kernels, share_ids(): pl.pallas_call(ids_kernel, out_shape=jax.ShapeDtypeStruct((GROUPS, 1, 128...  12 us

profile of v1, /device:TPU:1, one launch (start us, length us, event | category | flops | bytes accessed | tf_op | source)
XLA Modules:
  0.0 238.2 jit_solution(10130204739047339635)
XLA Ops:
  1.3 0.8 reshape.936
  2.0 1.3 concatenate.68
  3.4 12.0 %share_ids.1 = s32[32,1,128]{2,1,0:T(1,128)} custom-call(s32[1,128]{1,0:T(1,128)} %bitcast.187), custom_call_target="tpu_custom_call" | custom-call | tf_op jit(solution)/shard_map/share_ids/pallas_call | solution.py:303
  15.4 0.8 slice.157
  16.2 0.1 gt.15
  16.3 0.1 broadcast_in_dim_reshape.4
  16.4 0.2 convert_reduce_fusion.5
  16.6 0.1 select_reduce_fusion.1
  17.1 0.2 convert_reduce_fusion.6
  17.2 0.2 select_reduce_fusion.3
  17.4 0.6 compare_reduce_fusion
  18.6 0.3 copy-done.8
  18.9 0.2 copy-done.9
  20.1 0.8 fusion.105
  21.1 0.1 broadcast_in_dim_reshape.5
  21.3 0.8 reshape.941
  22.2 0.6 eq.246
  22.8 0.7 eq.245
  23.5 0.8 convolution_convert_fusion.3
  24.4 0.6 fusion.93
  25.0 0.8 and_reduce_fusion
  25.9 1.1 convert_reduce_fusion.4
  26.9 0.7 fusion.95
  28.9 0.5 fusion.70
  29.4 0.7 pad_maximum_fusion.2
  30.1 0.8 pad_maximum_fusion.1
  30.9 0.6 rem.117
  31.5 205.5 %conditional.1 = ((f32[32,1024]{1,0:T(8,128)S(1)}, f32[1,16]{1,0:T(1,128)S(1)})) conditional(s32[]{:T(128)} %convert_element_type.216, (s32[2,1]{0,1:T(1,128)}, s32[2,32]{1,0:T(2,128)}, s32[1,32]{1,0:T(1,128)}, bf16[2004,1024]{1,0:T(8,128)(2,1)}, s32[2]{0:T(128)}, /*index=5*/s32[1]{0:T(128)}, bf16[1,4096,1024]{2,1,0:T(8,128)(2,1)}, ...), branch_computations={%region_11.26_spmd, %region_26.29_spmd} | conditional | flops 2090632832 | bytes 152036992 | solution.py:923
  31.5 0.1 reduce_sum.199
  31.7 1.0 fusion.64
  32.7 1.2 broadcast_in_dim.322.episode_ref
  34.0 0.7 copy.101.count_ref
  34.6 1.3 dynamic_slice.57
  35.9 0.7 broadcast_in_dim.314
  36.6 0.7 broadcast_in_dim.312
  37.3 0.7 broadcast_in_dim.310
  38.0 0.7 select_bitcast_fusion
  39.0 1.1 select_reduce_fusion
  40.3 0.1 and_select_fusion.bias_ref
  40.4 0.2 select_n.351.slot_ref
  40.6 3.7 %gather_fusion = bf16[128,1024]{1,0:T(8,128)(2,1)S(1)} fusion(bf16[2004,1024]{1,0:T(8,128)(2,1)} %get-tuple-element.544, s32[1024]{0:T(1024)S(1)} %pad_clamp_fusion), kind=kCustom, calls=%fused_computation.1 | custom fusion | bytes 524800 | tf_op jit(solution)/shard_map/cond/branch_1_fun/jit(_take)/gather | solution.py:908
  44.5 92.2 %trunk.1.hid_ref = bf16[4,64,1024]{2,1,0:T(8,128)(2,1)S(1)} custom-call(bf16[8,16,1024]{2,1,0:T(8,128)(2,1)S(1)} %broadcast_select_fusion.rows_ref, s32[4,64,1]{2,1,0:T(8,128)S(1)} %select_n.351.slot_ref, f32[4,64,128]{2,1,0:T(8,128)S(1)} %copy-done.6, f32[4,64,128]{2,1,0:T(8,128)S(1)} %copy-done.5, f32[4,64,64]{2,1,0:T(8,128)S(1)} %and_select_fusion.bias_ref, ...), custom_call_target="tpu_custom_call" | custom-call | tf_op jit(solution)/shard_map/cond/branch_1_fun/trunk/pallas_call | solution.py:562
  136.8 0.8 copy-done
  137.5 0.4 copy.115
  138.0 0.6 and_select_fusion.1.weight_ref
  138.7 98.4 %close.1 = (f32[32,1024]{1,0:T(8,128)S(1)}, f32[1,16]{1,0:T(1,128)S(1)}) custom-call(bf16[4,64,1024]{2,1,0:T(8,128)(2,1)} %copy-done, f32[64,256]{1,0:T(8,128)} %and_select_fusion.1.weight_ref, f32[1,1024]{1,0:T(1,128)} %bitcast.178, f32[8,1]{1,0:T(8,128)} %copy.101.count_ref, s32[1,16]{1,0:T(1,128)} %broadcast_in_dim.322.episode_ref), custom_call_target="tpu_custom_call" | custom-call | tf_op jit(solution)/shard_map/cond/branch_1_fun/close/pallas_call | solution.py:730
  237.0 0.7 copy.174
  237.7 0.5 copy.175
  (81 shorter events, 3.1 us)
Async XLA Ops:
  17.0 3.1 %copy-start.10 = (s32[32]{0:T(128)}, s32[32]{0:T(128)S(1)}, u32[]{:S(2)}) copy-start(s32[32]{0:T(128)S(1)} %get-tuple-element.855) | copy-start | bytes 388
  17.1 2.9 %copy-start.13 = (s32[32]{0:T(128)}, s32[32]{0:T(128)S(1)}, u32[]{:S(2)}) copy-start(s32[32]{0:T(128)S(1)} %rev.8) | copy-start | bytes 388
  17.4 2.5 %copy-start.11 = (s32[32]{0:T(128)}, s32[32]{0:T(128)S(1)}, u32[]{:S(2)}) copy-start(s32[32]{0:T(128)S(1)} %get-tuple-element.799) | copy-start | bytes 388
  18.3 0.6 copy-start.8
  18.5 0.6 copy-start.9
  31.5 13.0 %copy-start.2 = (bf16[1,4096,256]{2,1,0:T(8,128)(2,1)S(1)}, bf16[1,4096,256]{2,1,0:T(8,128)(2,1)}, u32[]{:S(2)}) copy-start(bf16[1,4096,256]{2,1,0:T(8,128)(2,1)} %get-tuple-element.560.wk_ref) | copy-start | bytes 6291460 | tf_op jit(solution)/shard_map/cond
  31.5 13.0 %copy-start.4 = (f32[1,4096]{1,0:T(1,128)S(1)}, f32[1,4096]{1,0:T(1,128)}, u32[]{:S(2)}) copy-start(f32[1,4096]{1,0:T(1,128)} %get-tuple-element.558.gain_ref) | copy-start | bytes 49156 | tf_op jit(solution)/shard_map/cond
  31.5 13.0 %copy-start.5 = (f32[4,64,128]{2,1,0:T(8,128)S(1)}, f32[4,64,128]{2,1,0:T(8,128)}, u32[]{:S(2)}) copy-start(f32[4,64,128]{2,1,0:T(8,128)} %get-tuple-element.551.sin_ref) | copy-start | bytes 393220 | tf_op jit(solution)/shard_map/cond
  31.5 13.0 %copy-start.6 = (f32[4,64,128]{2,1,0:T(8,128)S(1)}, f32[4,64,128]{2,1,0:T(8,128)}, u32[]{:S(2)}) copy-start(f32[4,64,128]{2,1,0:T(8,128)} %get-tuple-element.550.cos_ref) | copy-start | bytes 393220 | tf_op jit(solution)/shard_map/cond
  44.5 93.5 %copy-start.7 = (s32[64,256]{1,0:T(8,128)S(1)}, s32[64,256]{1,0:T(8,128)}, u32[]{:S(2)}) copy-start(s32[64,256]{1,0:T(8,128)} %get-tuple-element.564) | copy-start | bytes 196612 | tf_op jit(solution)/shard_map/cond
  136.7 0.8 copy-start
